TPU v7x, 64 devices: a 2x2x8 block of a 4x4x8 slice. The times are simulated.
64 devices in a mesh: replica: 4 (over x, y), data: 16 (over z, core).
Axes of the slice: x: 2, y: 2, z: 8, core: 2. Of those that a mesh axis runs over, the one named last changes fastest.
The devices are a block of a 4x4x8 slice.
Arguments:
- q_hidden: bfloat16 [512, 20, 1536], P(('replica', 'data')), parts along dimension 0
- d_hidden: bfloat16 [512, 768, 1536], P(('replica', 'data')), parts along dimension 0
- w_proj: bfloat16 [1536, 128], replicated
- q_mask: int32 [512, 20], P(('replica', 'data')), parts along dimension 0
- d_mask: int32 [512, 768], P(('replica', 'data')), parts along dimension 0
- temperature: float32 [], replicated
Outputs:
- output 1: float32 [512], P(('replica', 'data')), parts along dimension 0
- output 2: float32 [512], P(('replica', 'data')), parts along dimension 0
- output 3: float32 [4], P('replica'), parts along dimension 0
There are 4 independent parts. A program takes and returns all parts, laid end to end along the dimension named above; an argument that names none is the same for every part.
All inputs are finite; a program needn't handle non-finite values.
Results may differ from a plain program's by a relative error of at most 0.001.
Values are sent between devices in bfloat16 or wider.
A program may use at most 768 MiB of HBM per device.

v0:
```python
import functools
import jax
import jax.numpy as jnp
from jax import lax
from jax.sharding import PartitionSpec as P

TILE_ELEMS = 8388608


def project(hidden, w_proj):
    raw_proj = jnp.einsum('bth,hk->btk', hidden, w_proj, preferred_element_type=jnp.float32)
    return (raw_proj / jnp.sqrt(jnp.sum(raw_proj * raw_proj, axis=-1, keepdims=True))).astype(jnp.bfloat16)


def blocks_per_step(total_blocks, block_elems):
    chosen = 1
    for candidate in range(1, total_blocks + 1):
        if total_blocks % candidate == 0 and candidate * block_elems <= TILE_ELEMS:
            chosen = candidate
    return chosen


def maxsim(q_vecs, p_vecs, d_mask):
    sim_vals = jnp.einsum('itk,jsk->itjs', q_vecs, p_vecs, preferred_element_type=jnp.float32)
    best_sim = jnp.max(jnp.where(d_mask[None, None, :, :] == 1, sim_vals, -jnp.inf), axis=3)
    return jnp.sum(best_sim, axis=1)


def solution(mesh):
    group_size = mesh.shape['data']
    batch_spec = P(('replica', 'data'))

    def local_loss(q_hidden, d_hidden, w_proj, q_mask, d_mask, value_a11):
        local_pairs = q_hidden.shape[0]
        q_len = q_hidden.shape[1]
        d_len = d_hidden.shape[1]
        proj_dim = w_proj.shape[1]
        q_vecs = jnp.where(q_mask[:, :, None] == 1, project(q_hidden, w_proj), 0.0).astype(jnp.bfloat16)
        p_vecs = project(d_hidden, w_proj)
        q_group = lax.all_gather(q_vecs, 'data', tiled=True)
        step_blocks = blocks_per_step(group_size, local_pairs * local_pairs * q_len * d_len)
        q_steps = q_group.reshape(group_size // step_blocks, step_blocks * local_pairs, q_len, proj_dim)
        col_scores = lax.map(functools.partial(maxsim, p_vecs=p_vecs, d_mask=d_mask), q_steps)
        col_scores = col_scores.reshape(group_size * local_pairs, local_pairs)
        row_scores = lax.all_to_all(col_scores, 'data', 0, 1, tiled=True)
        my_index = lax.axis_index('data')
        own_block = lax.dynamic_slice_in_dim(col_scores, my_index * local_pairs, local_pairs, axis=0)
        pos_logit = jnp.diagonal(own_block) / value_a11
        loss_query = jax.nn.logsumexp(row_scores / value_a11, axis=1) - pos_logit
        loss_doc = jax.nn.logsumexp(col_scores / value_a11, axis=0) - pos_logit
        group_sum = lax.psum(jnp.sum(loss_query + loss_doc), 'data')
        loss_mean = (group_sum / (2 * group_size * local_pairs)).reshape(1)
        return loss_query, loss_doc, loss_mean

    return jax.shard_map(local_loss, mesh=mesh, in_specs=(batch_spec, batch_spec, P(), batch_spec, batch_spec, P()), out_specs=(batch_spec, batch_spec, P('replica')), check_vma=False)
```

profile of v0, /device:TPU:21, one launch (start us, length us, event | category | flops | bytes accessed | tf_op | source)
XLA Modules:
  0.0 94.8 jit_solution(2477103773508977116)
XLA Ops:
  0.6 0.0 copy-start
  0.7 14.3 %multiply_reduce_fusion = (f32[8,768]{1,0:T(8,128)S(1)}, f32[8,768,128]{1,2,0:T(8,128)}) fusion(bf16[8,768,1536]{2,1,0:T(8,128)(2,1)} %param.9, bf16[1536,128]{1,0:T(8,128)(2,1)} %param.10), kind=kOutput, calls=%fused_computation.9 | convolution fusion | flops 2417485824 | bytes 22437888 | tf_op jit(solution)/shard_map/bth,hk->btk/dot_general | solution.py:11
  15.0 0.0 copy-start.1
  15.0 2.2 %divide_convert_fusion = bf16[8,768,128]{1,2,0:T(8,128)(2,1)S(1)} fusion(f32[8,768,128]{1,2,0:T(8,128)} %get-tuple-element.62, f32[8,768]{1,0:T(8,128)S(1)} %sqrt.17), kind=kLoop, calls=%fused_computation.8 | loop fusion | flops 1572864 | bytes 4743168 | tf_op jit(solution)/shard_map/convert_element_type | solution.py:12
  17.2 0.0 copy-start.3
  17.2 0.0 copy-start.2
  17.2 1.6 %copy.23 = bf16[8,768,128]{2,1,0:T(8,128)(2,1)} copy(bf16[8,768,128]{1,2,0:T(8,128)(2,1)S(1)} %divide_convert_fusion) | data formatting | bytes 3145728 | tf_op jit(solution)/shard_map/while | solution.py:43
  18.8 0.0 copy-done
  18.8 0.0 copy-done.1
  18.8 0.4 multiply_reduce_fusion.1
  19.2 0.0 copy-done.3
  19.2 0.1 copy.20
  19.3 0.1 fusion.8
  19.4 24.5 %all_gather.3 = bf16[128,20,128]{2,0,1:T(8,128)(2,1)S(1)} all-gather(bf16[8,20,128]{2,0,1:T(8,128)(2,1)S(1)} %fusion.8), channel_id=1, replica_groups=mesh['replica'=4,'data'=16] {'data'}, dimensions={0}, use_global_device_ids=true | all-gather | bytes 696320 | tf_op jit(solution)/shard_map/all_gather | solution.py:40
  44.0 0.0 copy-done.2
  44.0 12.2 %while.10 = (s32[]{:T(128)}, f32[2,64,8]{1,2,0:T(8,128)S(1)}, s32[8,768]{1,0:T(8,128)S(1)}, bf16[2,64,20,128]{3,1,0,2:T(8,128)(2,1)S(1)}, bf16[8,768,128]{2,1,0:T(8,128)(2,1)}, /*index=5*/s32[]{:T(128)}, f32[]{:T(128)}) while((s32[]{:T(128)}, f32[2,64,8]{1,2,0:T(8,128)S(1)}, s32[8,768]{1,0:T(8,128)S(1)}, ...), condition=%wide.region_5.6_spmd, body=%wide.region_2.5_spmd.sunk | while | flops 2029000192 | bytes 2029657 | solution.py:43
  44.0 6.0 %select_reduce_fusion.2 = f32[64,20,8]{0,2,1:T(8,128)S(1)} fusion(pred[8,768]{1,0:T(8,128)(4,1)S(1)} %broadcast_compare_fusion.3, bf16[8,768,128]{2,1,0:T(8,128)(2,1)} %get-tuple-element.112, bf16[2,64,20,128]{3,1,0,2:T(8,128)(2,1)S(1)} %get-tuple-element.111, s32[]{:T(128)} %get-tuple-element.101), kind=kOutput, calls=%fused_computation.1.clone.1 | convolution fusion | flops 2028984320 | bytes 1947652 | tf_op jit(solution)/shard_map/while/body/eval_jaxpr/itk,jsk->itjs/dot_general | solution.py:24
  50.1 6.0 %select_reduce_fusion.2 = f32[64,20,8]{0,2,1:T(8,128)S(1)} fusion(pred[8,768]{1,0:T(8,128)(4,1)S(1)} %broadcast_compare_fusion.3, bf16[8,768,128]{2,1,0:T(8,128)(2,1)} %get-tuple-element.112, bf16[2,64,20,128]{3,1,0,2:T(8,128)(2,1)S(1)} %get-tuple-element.111, s32[]{:T(128)} %get-tuple-element.101), kind=kOutput, calls=%fused_computation.1.clone.1 | convolution fusion | flops 2028984320 | bytes 1947652 | tf_op jit(solution)/shard_map/while/body/eval_jaxpr/itk,jsk->itjs/dot_general | solution.py:24
  56.1 0.1 all_to_all.10
  56.2 0.6 copy.25
  56.9 3.7 %all-to-all-start = ((f32[16,8,8]{1,2,0:T(8,128)}), f32[16,8,8]{1,2,0:T(8,128)S(1)}, u32[]{:S(2)}, u32[]{:S(2)}) async-start(f32[16,8,8]{1,2,0:T(8,128)} %copy.25), calls=%async_computation | async-start | bytes 131072 | tf_op jit(solution)/shard_map/all_to_all | solution.py:45
  60.5 0.1 copy.31
  61.3 0.1 fusion.10
  61.4 0.2 exponential_reduce_fusion.1
  61.6 0.6 gather_fusion
  62.3 5.5 %all-to-all-done = f32[16,8,8]{1,2,0:T(8,128)S(1)} async-done(((f32[16,8,8]{1,2,0:T(8,128)}), f32[16,8,8]{1,2,0:T(8,128)S(1)}, u32[]{:S(2)}, u32[]{:S(2)}) %all-to-all-start) | async-done | bytes 4128 | tf_op jit(solution)/shard_map/all_to_all | solution.py:45
  67.9 1.1 %add_reduce_fusion = (f32[]{:T(128)}, f32[8]{0:T(128)}, f32[8]{0:T(128)}) fusion(f32[8]{0:T(128)S(1)} %fusion.10, f32[8]{0:T(128)S(1)} %exponential_reduce_fusion.1, f32[8]{0:T(128)S(1)} %fusion.9, f32[8]{0:T(128)S(1)} %exponential_reduce_fusion, f32[8]{0:T(128)S(1)} %gather_fusion, f32[]{:T(128)S(6)} %copy.41), kind=kLoop, calls=%fused_computation.27 | loop fusion | flops 103 | bytes 232 | tf_op jit(solution)/shard_map/reduce_sum | solution.py:51
  69.0 23.9 %psum.7 = f32[]{:T(128)} all-reduce(f32[]{:T(128)} %get-tuple-element.56), channel_id=1, replica_groups=mesh['replica'=4,'data'=16] {'data'}, use_global_device_ids=true, to_apply=%region_11.12 | all-reduce | flops 1 | bytes 8 | tf_op jit(solution)/shard_map/psum | solution.py:51
  (17 shorter events, 0.2 us)
Async XLA Ops:
  0.6 18.2 %copy-start = (bf16[8,20,1536]{2,0,1:T(8,128)(2,1)S(1)}, bf16[8,20,1536]{2,0,1:T(8,128)(2,1)}, u32[]{:S(2)}) copy-start(bf16[8,20,1536]{2,0,1:T(8,128)(2,1)} %param.8) | copy-start | bytes 1474564
  15.0 3.8 %copy-start.1 = (bf16[1536,128]{1,0:T(8,128)(2,1)S(1)}, bf16[1536,128]{1,0:T(8,128)(2,1)}, u32[]{:S(2)}) copy-start(bf16[1536,128]{1,0:T(8,128)(2,1)} %param.10) | copy-start | bytes 1179652
  17.2 2.0 %copy-start.3 = (s32[8,20]{1,0:T(8,128)S(1)}, s32[8,20]{1,0:T(8,128)}, u32[]{:S(2)}) copy-start(s32[8,20]{1,0:T(8,128)} %param.11) | copy-start | bytes 1924
  17.2 26.8 %copy-start.2 = (s32[8,768]{1,0:T(8,128)S(1)}, s32[8,768]{1,0:T(8,128)}, u32[]{:S(2)}) copy-start(s32[8,768]{1,0:T(8,128)} %param.12) | copy-start | bytes 73732
  56.9 10.9 %all-to-all-start = ((f32[16,8,8]{1,2,0:T(8,128)}), f32[16,8,8]{1,2,0:T(8,128)S(1)}, u32[]{:S(2)}, u32[]{:S(2)}) async-start(f32[16,8,8]{1,2,0:T(8,128)} %copy.25), calls=%async_computation | async-start | bytes 131072 | tf_op jit(solution)/shard_map/all_to_all | solution.py:45
where the time goes:
time: 95 us; the launch traced here: 94.8 us
  blocking collectives  48.4 us (51%)
  matrix products  26.7 us (28%)
  waiting for transfers between devices  5.55 us (6%)
  other arithmetic  3.91 us (4%)
  starting transfers between devices  3.66 us (4%)
  between operations  3.23 us (3%)
  local copies, waits for them, and re-layouts  3.21 us (3%)
    all_gather x1, blocking collectives, local_loss(): q_group = lax.all_gather(q_vecs, 'data', tiled=True)  24.5 us
    psum x1, blocking collectives, local_loss(): group_sum = lax.psum(jnp.sum(loss_query + loss_doc), 'data')  23.9 us
    dot_general x2, matrix products, project(): jnp.einsum('bth,hk->btk', hidden, w_proj, preferred_element_type=jnp.floa...  14.7 us
    dot_general x2, matrix products, maxsim(): jnp.einsum('itk,jsk->itjs', q_vecs, p_vecs, preferred_element_type=jnp.fl...  12 us
    all_to_all x1, waiting for transfers between devices, local_loss(): row_scores = lax.all_to_all(col_scores, 'data', 0, 1, tiled=True)  5.55 us
    all_to_all x1, starting transfers between devices, local_loss(): row_scores = lax.all_to_all(col_scores, 'data', 0, 1, tiled=True)  3.66 us
    convert_element_type x1, other arithmetic, project(): (raw_proj / jnp.sqrt(jnp.sum(raw_proj * raw_proj, axis=-1, keepdims=True)...  2.19 us
  transfers between devices with their start and end apart: 1, of which 1 were waited for; matrix products, arithmetic and copies ran while one was open for 1% of the time, Pallas kernels for 0%

commit v1 on v0

v1 whole, which is shorter than its diff:
```python
import functools

import jax
import jax.numpy as jnp
from jax import lax
from jax.experimental import pallas as pl
from jax.experimental.pallas import tpu as pltpu
from jax.sharding import PartitionSpec as P

MESH = pl.DeviceIdType.MESH
CORES = 2
ROWS = 256
COLS = 256
BIG = 2.0 ** 100


def chip_offsets(chips):
    order = [0]
    for dist in range(1, chips // 2 + 1):
        order.append(dist)
        if 2 * dist != chips:
            order.append(-dist)
    return order


def normalise(raw):
    return raw * lax.rsqrt(jnp.sum(raw * raw, axis=-1, keepdims=True))


def kernel(group, temp_ref, q_hbm, d_hbm, w_hbm, qm_ref, dm_ref, lq_ref, ld_ref, lm_ref,
           q_in, d_in, w_in, q_buf, p_buf, bias, best, fin,
           q_sem, w_sem, d_sem, q_send, q_recv, relay_send, fin_send, fin_recv):
    pairs, q_len, hidden = q_in.shape
    d_len = dm_ref.shape[1]
    dim = w_in.shape[1]
    block = pairs * q_len
    chips = group // CORES
    offsets = chip_offsets(chips)
    tokens = group * block
    queries = group * pairs
    doc_rows = pairs * d_len
    tiles = doc_rows // ROWS

    me = lax.axis_index('data')
    chip = lax.div(me, CORES)
    core = lax.rem(me, CORES)
    partner = chip * CORES + (CORES - 1 - core)

    def at_offset(off):
        return lax.rem(chip + off + chips, chips)

    q_copy = pltpu.make_async_copy(q_hbm, q_in, q_sem)
    w_copy = pltpu.make_async_copy(w_hbm, w_in, w_sem)
    q_copy.start()
    w_copy.start()

    def d_copy(i):
        rows = pl.ds(pl.multiple_of(i * ROWS, ROWS), ROWS)
        return pltpu.make_async_copy(d_hbm.at[rows], d_in.at[rows], d_sem.at[i])

    for i in range(tiles):
        d_copy(i).start()

    barrier = pltpu.get_barrier_semaphore()
    for step in range(1, group):
        pl.semaphore_signal(barrier, inc=1, device_id={'data': lax.rem(me + step, group)}, device_id_type=MESH)

    row_pair = lax.broadcasted_iota(jnp.int32, (block, pairs), 0) // q_len
    picks = (row_pair == lax.broadcasted_iota(jnp.int32, (block, pairs), 1)).astype(jnp.bfloat16)
    spread = jnp.dot(picks, qm_ref[...].astype(jnp.float32).astype(jnp.bfloat16), preferred_element_type=jnp.float32)
    row_step = lax.broadcasted_iota(jnp.int32, (block, q_len), 0) % q_len
    own_step = row_step == lax.broadcasted_iota(jnp.int32, (block, q_len), 1)
    q_keep = jnp.sum(jnp.where(own_step, spread, 0.0), axis=1, keepdims=True)
    doc_bias = jnp.where(dm_ref[...] == 1, 0.0, -BIG)
    doc_bias = jnp.transpose(jnp.concatenate([doc_bias, jnp.zeros((128 - pairs, d_len), jnp.float32)], axis=0))
    for j in range(pairs):
        bias[j * d_len:(j + 1) * d_len, :] = jnp.broadcast_to(doc_bias[:, j:j + 1], (d_len, dim)).astype(jnp.bfloat16)

    q_copy.wait()
    w_copy.wait()
    q_raw = jnp.dot(q_in[...].reshape(block, hidden), w_in[...], preferred_element_type=jnp.float32)
    q_buf[0:block, :] = jnp.where(q_keep > 0.5, normalise(q_raw), 0.0).astype(jnp.bfloat16)

    def project(i):
        d_copy(i).wait()
        rows = pl.ds(pl.multiple_of(i * ROWS, ROWS), ROWS)
        raw = jnp.dot(d_in[rows, :], w_in[...], preferred_element_type=jnp.float32)
        p_buf[rows, :] = normalise(raw).astype(jnp.bfloat16)

    project(0)
    pl.semaphore_wait(barrier, group - 1)

    def slot(s):
        return q_buf.at[pl.ds(s * block, block), :]

    def to_partner():
        return pltpu.make_async_remote_copy(slot(0), slot(1), q_send.at[0], q_recv.at[1],
                                            device_id={'data': partner}, device_id_type=MESH)

    def to_chip(k):
        back = offsets.index(-offsets[k]) if -offsets[k] in offsets else k
        return pltpu.make_async_remote_copy(slot(0), slot(2 * back), q_send.at[k], q_recv.at[2 * back],
                                            device_id={'data': at_offset(offsets[k]) * CORES + core}, device_id_type=MESH)

    def relay(k):
        return pltpu.make_async_remote_copy(slot(2 * k), slot(2 * k + 1), relay_send.at[k], q_recv.at[2 * k + 1],
                                            device_id={'data': partner}, device_id_type=MESH)

    def arrival(s):
        return pltpu.make_async_remote_copy(slot(s), slot(s), q_send.at[0], q_recv.at[s],
                                            device_id={'data': partner}, device_id_type=MESH)

    to_partner().start()
    for k in range(1, chips):
        to_chip(k).start()

    def project_body(i, carry):
        project(i)
        return carry

    lax.fori_loop(1, tiles, project_body, 0)

    ones = (lax.broadcasted_iota(jnp.int32, (COLS, dim), 1) == 0).astype(jnp.bfloat16)
    ready = 1
    for n in range(tokens // COLS):
        last = (COLS * (n + 1) - 1) // block
        while ready <= last:
            arrival(ready).wait_recv()
            if ready % 2 == 0:
                relay(ready // 2).start()
            ready += 1
        rhs = jnp.concatenate([q_buf[n * COLS:(n + 1) * COLS, :], ones], axis=1)

        def score(j, carry):
            rows = pl.ds(pl.multiple_of(j * d_len, d_len), d_len)
            lhs = jnp.concatenate([p_buf[rows, :], bias[rows, :]], axis=1)
            sim = lax.dot_general(lhs, rhs, (((1,), (1,)), ((), ())), preferred_element_type=jnp.float32)
            best[pl.ds(j, 1), n * COLS:(n + 1) * COLS] = jnp.max(sim, axis=0, keepdims=True)
            return carry

        lax.fori_loop(0, pairs, score, 0)

    scores = jnp.zeros((pairs, queries), jnp.float32)
    for n in range(tokens // COLS):
        row = lax.broadcasted_iota(jnp.int32, (COLS, queries), 0) + n * COLS
        first, last = n * COLS // block, (COLS * (n + 1) - 1) // block
        start = None
        for s in range(first, last + 1):
            owner = at_offset(offsets[s // 2]) * CORES + (core if s % 2 == 0 else CORES - 1 - core)
            shift = owner * pairs - s * pairs
            start = shift if start is None else jnp.where(row >= s * block, shift, start)
        query = row // q_len + start
        picks = (query == lax.broadcasted_iota(jnp.int32, (COLS, queries), 1)).astype(jnp.bfloat16)
        part = best[:, n * COLS:(n + 1) * COLS]
        high = part.astype(jnp.bfloat16)
        rest = part - high.astype(jnp.float32)
        mid = rest.astype(jnp.bfloat16)
        low = (rest - mid.astype(jnp.float32)).astype(jnp.bfloat16)
        for piece in (low, mid, high):
            scores += jnp.dot(piece, picks, preferred_element_type=jnp.float32)

    z = scores / temp_ref[0]
    lane = lax.broadcasted_iota(jnp.int32, (pairs, queries), 1)
    sub = lax.broadcasted_iota(jnp.int32, (pairs, queries), 0)
    pos_grid = jnp.where(lane == me * pairs + sub, z, 0.0)
    pos_col = jnp.sum(pos_grid, axis=1, keepdims=True)
    pos_row = jnp.sum(pos_grid, axis=0, keepdims=True)
    col_max = jnp.max(z, axis=1, keepdims=True)
    lse_doc = jnp.log(jnp.sum(jnp.exp(z - col_max), axis=1, keepdims=True)) + col_max
    loss_doc = lse_doc - pos_col
    row_max = jnp.max(z, axis=0, keepdims=True)
    row_sum = jnp.sum(jnp.exp(z - row_max), axis=0, keepdims=True)
    doc_part = jnp.broadcast_to(jnp.sum(loss_doc - pos_col, axis=0, keepdims=True), (1, queries))
    fin[me] = jnp.concatenate([row_max, row_sum, doc_part, doc_part], axis=0)

    def share(step):
        to = lax.rem(me + step, group)
        return pltpu.make_async_remote_copy(fin.at[me], fin.at[me], fin_send.at[step - 1], fin_recv.at[step - 1],
                                            device_id={'data': to}, device_id_type=MESH)

    def shared(step):
        source = lax.rem(me - step + group, group)
        return pltpu.make_async_remote_copy(fin.at[source], fin.at[source], fin_send.at[step - 1], fin_recv.at[step - 1],
                                            device_id={'data': source}, device_id_type=MESH)

    for step in range(1, group):
        share(step).start()

    ld_ref[...] = jnp.sum(jnp.where(lane == sub, loss_doc, 0.0), axis=0, keepdims=True)[:, :pairs]

    to_partner().wait_send()
    for k in range(1, chips):
        to_chip(k).wait_send()
        relay(k).wait_send()
    for step in range(1, group):
        shared(step).wait_recv()

    every = fin[...]
    maxes, sums = every[:, 0, :], every[:, 1, :]
    top = jnp.max(maxes, axis=0, keepdims=True)
    lse_query = jnp.log(jnp.sum(sums * jnp.exp(maxes - top), axis=0, keepdims=True)) + top
    loss_query = lse_query - pos_row
    own = jnp.where(lane == me * pairs + sub, loss_query, 0.0)
    own = jnp.sum(own, axis=1, keepdims=True)
    lq_ref[...] = jnp.sum(jnp.where(lane == sub, own, 0.0), axis=0, keepdims=True)[:, :pairs]
    total = jnp.sum(lse_query, axis=1, keepdims=True) + jnp.sum(every[:, 2, :], axis=0, keepdims=True)[:, :1]
    lm_ref[...] = total / (2 * queries)

    for step in range(1, group):
        share(step).wait_send()


def solution(mesh):
    group = mesh.shape['data']
    batch_spec = P(('replica', 'data'))

    def local_loss(q_hidden, d_hidden, w_proj, q_mask, d_mask, temperature):
        pairs, q_len, hidden = q_hidden.shape
        d_len = d_hidden.shape[1]
        dim = w_proj.shape[1]
        block = pairs * q_len
        chips = group // CORES
        vmem = pl.BlockSpec(memory_space=pltpu.VMEM)
        hbm = pl.BlockSpec(memory_space=pl.ANY)
        out = pl.pallas_call(
            functools.partial(kernel, group),
            out_shape=[jax.ShapeDtypeStruct((1, pairs), jnp.float32), jax.ShapeDtypeStruct((1, pairs), jnp.float32),
                       jax.ShapeDtypeStruct((1, 1), jnp.float32)],
            in_specs=[pl.BlockSpec(memory_space=pltpu.SMEM), hbm, hbm, hbm, vmem, vmem],
            out_specs=[vmem, vmem, vmem],
            scratch_shapes=[
                pltpu.VMEM((pairs, q_len, hidden), jnp.bfloat16),
                pltpu.VMEM((pairs * d_len, hidden), jnp.bfloat16),
                pltpu.VMEM((hidden, dim), jnp.bfloat16),
                pltpu.VMEM((group * block, dim), jnp.bfloat16),
                pltpu.VMEM((pairs * d_len, dim), jnp.bfloat16),
                pltpu.VMEM((pairs * d_len, dim), jnp.bfloat16),
                pltpu.VMEM((pairs, group * block), jnp.float32),
                pltpu.VMEM((group, 4, group * pairs), jnp.float32),
                pltpu.SemaphoreType.DMA,
                pltpu.SemaphoreType.DMA,
                pltpu.SemaphoreType.DMA((pairs * d_len // ROWS,)),
                pltpu.SemaphoreType.DMA((chips,)),
                pltpu.SemaphoreType.DMA((group,)),
                pltpu.SemaphoreType.DMA((chips,)),
                pltpu.SemaphoreType.DMA((group - 1,)),
                pltpu.SemaphoreType.DMA((group - 1,)),
            ],
            compiler_params=pltpu.CompilerParams(collective_id=0, has_side_effects=True, vmem_limit_bytes=56 * 2 ** 20),
            name='late_interaction',
        )(temperature.reshape(1), q_hidden, d_hidden.reshape(pairs * d_len, hidden), w_proj, q_mask, d_mask)
        return out[0].reshape(pairs), out[1].reshape(pairs), out[2].reshape(1)

    return jax.shard_map(local_loss, mesh=mesh, in_specs=(batch_spec, batch_spec, P(), batch_spec, batch_spec, P()),
                         out_specs=(batch_spec, batch_spec, P('replica')), check_vma=False)
```

time: 95 us -> 66.5 us (0.70)
  Pallas kernels: 0 us -> 59 us
  blocking collectives: 48.4 us -> 0 us
  matrix products: 26.7 us -> 0 us
  waiting for transfers between devices: 5.55 us -> 0 us
  other arithmetic: 3.91 us -> 0 us
  starting transfers between devices: 3.66 us -> 0 us
  local copies, waits for them, and re-layouts: 3.21 us -> 4.34 us
    pallas_call x0 -> x1, Pallas kernels: none -> 59 us  [local_loss(): pl.pallas_call(functools.partial(kernel, group), out_shape=[jax.ShapeDtyp...]
    dot_general x4 -> x0, matrix products: 26.7 us -> none  [the longest x2 14.7 us: project(): jnp.einsum('bth,hk->btk', hidden, w_proj, preferred_element_type=jnp.floa...]
    all_gather x1 -> x0, blocking collectives: 24.5 us -> none  [local_loss(): q_group = lax.all_gather(q_vecs, 'data', tiled=True)]
    psum x1 -> x0, blocking collectives: 23.9 us -> none  [local_loss(): group_sum = lax.psum(jnp.sum(loss_query + loss_doc), 'data')]
    all_to_all x1 -> x0, waiting for transfers between devices: 5.55 us -> none  [local_loss(): row_scores = lax.all_to_all(col_scores, 'data', 0, 1, tiled=True)]
    unnamed x8 -> x3, local copies, waits for them, and re-layouts: 0.03 us -> 4.34 us
    all_to_all x1 -> x0, starting transfers between devices: 3.66 us -> none  [local_loss(): row_scores = lax.all_to_all(col_scores, 'data', 0, 1, tiled=True)]
    convert_element_type x1 -> x0, other arithmetic: 2.19 us -> none  [project(): (raw_proj / jnp.sqrt(jnp.sum(raw_proj * raw_proj, axis=-1, keepdims=True)...]
  transfers between devices with their start and end apart: 1 -> 0, of which waited for: 1 -> 0; matrix products, arithmetic and copies ran while one was open for 1% -> 0% of each run, Pallas kernels for 0% -> 0%
where the time goes in v1:
time: 66.5 us; the launch traced here: 66.3 us
  Pallas kernels  59 us (89%)
  local copies, waits for them, and re-layouts  4.34 us (7%)
  between operations  2.98 us (4%)
    pallas_call x1, Pallas kernels, local_loss(): pl.pallas_call(functools.partial(kernel, group), out_shape=[jax.ShapeDtyp...  59 us
    unnamed x3, local copies, waits for them, and re-layouts  4.34 us

profile of v1, /device:TPU:21, one launch (start us, length us, event | category | flops | bytes accessed | tf_op | source)
XLA Modules:
  0.0 66.3 jit_solution(14192214399996251286)
XLA Ops:
  1.3 2.0 %copy.9.q_hbm = bf16[8,20,1536]{2,1,0:T(8,128)(2,1)} copy(bf16[8,20,1536]{2,0,1:T(8,128)(2,1)} %param.6) | data formatting | bytes 983040 | tf_op args[0]
  3.3 59.0 %late_interaction.1 = (f32[1,8]{1,0:T(1,128)}, f32[1,8]{1,0:T(1,128)}, f32[1,1]{1,0:T(1,128)}) custom-call(f32[1]{0:T(128)} %bitcast.5.temp_ref, bf16[8,20,1536]{2,1,0:T(8,128)(2,1)} %copy.9.q_hbm, bf16[6144,1536]{1,0:T(8,128)(2,1)} %bitcast.6, bf16[1536,128]{1,0:T(8,128)(2,1)} %w_hbm.1, s32[8,20]{1,0:T(8,128)} %qm_ref.1, s32[8,768]{1,0:T(8,128)} %dm_ref.1), custom_call_target="tpu_custom_call" | custom-call | tf_op jit(solution)/shard_map/late_interaction/pallas_call | solution.py:225
  62.3 1.2 %copy.14 = f32[8]{0:T(128)} copy(f32[8]{0:T(128)} %bitcast.8) | data formatting | bytes 64
  63.4 1.2 %copy.15 = f32[8]{0:T(128)} copy(f32[8]{0:T(128)} %bitcast.7) | data formatting | bytes 64

commit v2 on v1

v2 whole, which is shorter than its diff:
```python
import functools

import jax
import jax.numpy as jnp
from jax import lax
from jax.experimental import pallas as pl
from jax.experimental.pallas import tpu as pltpu
from jax.sharding import PartitionSpec as P

MESH = pl.DeviceIdType.MESH
CORES = 2
ROWS = 256
COLS = 256
BIG = 2.0 ** 100
EARLY = 2
GREET = 2
STEP = 2
LEAD = 2


def chip_offsets(chips):
    order = [0]
    for dist in range(1, chips // 2 + 1):
        order.append(dist)
        if 2 * dist != chips:
            order.append(-dist)
    return order


def normalise(raw):
    return raw * lax.rsqrt(jnp.sum(raw * raw, axis=-1, keepdims=True))


def kernel(group, temp_ref, q_hbm, d_hbm, w_hbm, qm_hbm, dm_hbm, lq_ref, ld_ref, lm_ref,
           q_in, d_in, w_in, qm_ref, dm_ref, q_buf, p_buf, bias, best, fin,
           q_sem, w_sem, qm_sem, dm_sem, d_sem, q_send, q_recv, relay_send, fin_send, fin_recv):
    pairs, q_len = qm_ref.shape
    hidden = q_in.shape[1]
    d_len = dm_ref.shape[1]
    dim = w_in.shape[1]
    block = pairs * q_len
    chips = group // CORES
    offsets = chip_offsets(chips)
    tokens = group * block
    queries = group * pairs
    doc_rows = pairs * d_len
    tiles = doc_rows // ROWS

    me = lax.axis_index('data')
    chip = lax.div(me, CORES)
    core = lax.rem(me, CORES)
    partner = chip * CORES + (CORES - 1 - core)

    def at_offset(off):
        return lax.rem(chip + off + chips, chips)

    w_copy = pltpu.make_async_copy(w_hbm, w_in, w_sem)
    q_copy = pltpu.make_async_copy(q_hbm, q_in, q_sem)
    qm_copy = pltpu.make_async_copy(qm_hbm, qm_ref, qm_sem)
    dm_copy = pltpu.make_async_copy(dm_hbm, dm_ref, dm_sem)

    def d_copy(i):
        rows = pl.ds(i * ROWS, ROWS)
        return pltpu.make_async_copy(d_hbm.at[rows], d_in.at[rows], d_sem.at[i])

    for copy in (qm_copy, w_copy, q_copy, dm_copy):
        copy.start()
    for i in range(EARLY):
        d_copy(i).start()

    barrier = pltpu.get_barrier_semaphore()
    for step in range(1, group):
        pl.semaphore_signal(barrier, inc=1, device_id={'data': lax.rem(me + step, group)}, device_id_type=MESH)

    with jax.named_scope('qmask'):
        qm_copy.wait()
        row_pair = lax.broadcasted_iota(jnp.int32, (block, pairs), 0) % pairs
        picks = (row_pair == lax.broadcasted_iota(jnp.int32, (block, pairs), 1)).astype(jnp.bfloat16)
        spread = jnp.dot(picks, qm_ref[...].astype(jnp.float32).astype(jnp.bfloat16), preferred_element_type=jnp.float32)
        row_step = lax.broadcasted_iota(jnp.int32, (block, q_len), 0) // pairs
        own_step = row_step == lax.broadcasted_iota(jnp.int32, (block, q_len), 1)
        q_keep = jnp.sum(jnp.where(own_step, spread, 0.0), axis=1, keepdims=True)
    with jax.named_scope('qproj'):
        w_copy.wait()
        q_copy.wait()
        for i in range(EARLY, tiles):
            d_copy(i).start()
        q_raw = jnp.dot(q_in[...], w_in[...], preferred_element_type=jnp.float32)
        q_buf[0:block, :] = jnp.where(q_keep > 0.5, normalise(q_raw), 0.0).astype(jnp.bfloat16)

    def project(i):
        rows = pl.ds(i * ROWS, ROWS)
        raw = jnp.dot(d_in[rows, :], w_in[...], preferred_element_type=jnp.float32)
        p_buf[rows, :] = normalise(raw).astype(jnp.bfloat16)

    def slot(s):
        return q_buf.at[pl.ds(s * block, block), :]

    def to_partner():
        return pltpu.make_async_remote_copy(slot(0), slot(1), q_send.at[0], q_recv.at[1],
                                            device_id={'data': partner}, device_id_type=MESH)

    def to_chip(k):
        back = offsets.index(-offsets[k]) if -offsets[k] in offsets else k
        return pltpu.make_async_remote_copy(slot(0), slot(2 * back), q_send.at[k], q_recv.at[2 * back],
                                            device_id={'data': at_offset(offsets[k]) * CORES + core}, device_id_type=MESH)

    def relay(k):
        return pltpu.make_async_remote_copy(slot(2 * k), slot(2 * k + 1), relay_send.at[k], q_recv.at[2 * k + 1],
                                            device_id={'data': partner}, device_id_type=MESH)

    def arrival(s):
        return pltpu.make_async_remote_copy(slot(s), slot(s), q_send.at[0], q_recv.at[s],
                                            device_id={'data': partner}, device_id_type=MESH)

    arrived = {0}

    def need(s):
        if s not in arrived:
            with jax.named_scope(f'need{s}'):
                arrival(s).wait_recv()
            arrived.add(s)

    def pass_on(k):
        need(2 * k)
        relay(k).start()

    with jax.named_scope('proj'):
        for i in range(tiles):
            if i == 1:
                with jax.named_scope('dmask'):
                    dm_copy.wait()
                    doc_bias = jnp.where(dm_ref[...] == 1, 0.0, -BIG)
                    doc_bias = jnp.concatenate([doc_bias, jnp.zeros((128 - pairs, d_len), jnp.float32)], axis=0)
                    doc_bias = jnp.transpose(doc_bias)
                    for j in range(pairs):
                        bias[j * d_len:(j + 1) * d_len, :] = jnp.broadcast_to(
                            doc_bias[:, j:j + 1], (d_len, dim)).astype(jnp.bfloat16)
            if i == GREET:
                with jax.named_scope('barrier'):
                    pl.semaphore_wait(barrier, group - 1)
                to_partner().start()
                for k in range(1, chips):
                    to_chip(k).start()
            if i % STEP == 0:
                for t in range(i, i + STEP):
                    d_copy(t).wait()
            project(i)
        pass_on(1)

    first_tile = [s * block // COLS for s in range(group)]
    ones = (lax.broadcasted_iota(jnp.int32, (COLS, dim), 1) == 0).astype(jnp.bfloat16)
    for n in range(tokens // COLS):
        for k in range(2, chips):
            if max(first_tile[2 * k + 1] - LEAD, 0) == n:
                pass_on(k)
        for s in range(group):
            if first_tile[s] == n:
                need(s)
        with jax.named_scope(f'score{n}'):
            rhs = jnp.concatenate([q_buf[n * COLS:(n + 1) * COLS, :], ones], axis=1)
            for j in range(0, pairs):
                rows = pl.ds(j * d_len, d_len)
                lhs = jnp.concatenate([p_buf[rows, :], bias[rows, :]], axis=1)
                sim = lax.dot_general(lhs, rhs, (((1,), (1,)), ((), ())), preferred_element_type=jnp.float32)
                best[pl.ds(j, 1), n * COLS:(n + 1) * COLS] = jnp.max(sim, axis=0, keepdims=True)

    with jax.named_scope('segsum'):
        scores = jnp.zeros((pairs, queries), jnp.float32)
        for n in range(tokens // COLS):
            row = lax.broadcasted_iota(jnp.int32, (COLS, queries), 0) + n * COLS
            first, last = n * COLS // block, (COLS * (n + 1) - 1) // block
            start = None
            for s in range(first, last + 1):
                owner = at_offset(offsets[s // 2]) * CORES + (core if s % 2 == 0 else CORES - 1 - core)
                start = owner * pairs if start is None else jnp.where(row >= s * block, owner * pairs, start)
            query = row % pairs + start
            picks = (query == lax.broadcasted_iota(jnp.int32, (COLS, queries), 1)).astype(jnp.bfloat16)
            part = best[:, n * COLS:(n + 1) * COLS]
            high = part.astype(jnp.bfloat16)
            rest = part - high.astype(jnp.float32)
            mid = rest.astype(jnp.bfloat16)
            low = (rest - mid.astype(jnp.float32)).astype(jnp.bfloat16)
            for piece in (low, mid, high):
                scores += jnp.dot(piece, picks, preferred_element_type=jnp.float32)

    with jax.named_scope('partial'):
        z = scores / temp_ref[0]
        lane = lax.broadcasted_iota(jnp.int32, (pairs, queries), 1)
        sub = lax.broadcasted_iota(jnp.int32, (pairs, queries), 0)
        pos_grid = jnp.where(lane == me * pairs + sub, z, 0.0)
        pos_col = jnp.sum(pos_grid, axis=1, keepdims=True)
        pos_row = jnp.sum(pos_grid, axis=0, keepdims=True)
        col_max = jnp.max(z, axis=1, keepdims=True)
        lse_doc = jnp.log(jnp.sum(jnp.exp(z - col_max), axis=1, keepdims=True)) + col_max
        loss_doc = lse_doc - pos_col
        row_max = jnp.max(z, axis=0, keepdims=True)
        row_sum = jnp.sum(jnp.exp(z - row_max), axis=0, keepdims=True)
        doc_part = jnp.broadcast_to(jnp.sum(loss_doc - pos_col, axis=0, keepdims=True), (1, queries))
        fin[me] = jnp.concatenate([row_max, row_sum, doc_part, doc_part], axis=0)

    def share(step):
        to = lax.rem(me + step, group)
        return pltpu.make_async_remote_copy(fin.at[me], fin.at[me], fin_send.at[step - 1], fin_recv.at[step - 1],
                                            device_id={'data': to}, device_id_type=MESH)

    def shared(step):
        source = lax.rem(me - step + group, group)
        return pltpu.make_async_remote_copy(fin.at[source], fin.at[source], fin_send.at[step - 1], fin_recv.at[step - 1],
                                            device_id={'data': source}, device_id_type=MESH)

    for step in range(1, group):
        share(step).start()

    ld_ref[...] = jnp.sum(jnp.where(lane == sub, loss_doc, 0.0), axis=0, keepdims=True)[:, :pairs]

    with jax.named_scope('shwait'):
        to_partner().wait_send()
        for k in range(1, chips):
            to_chip(k).wait_send()
            relay(k).wait_send()
        for step in range(1, group):
            shared(step).wait_recv()

    with jax.named_scope('finish'):
        every = fin[...]
        maxes, sums = every[:, 0, :], every[:, 1, :]
        top = jnp.max(maxes, axis=0, keepdims=True)
        lse_query = jnp.log(jnp.sum(sums * jnp.exp(maxes - top), axis=0, keepdims=True)) + top
        loss_query = lse_query - pos_row
        own = jnp.where(lane == me * pairs + sub, loss_query, 0.0)
        own = jnp.sum(own, axis=1, keepdims=True)
        lq_ref[...] = jnp.sum(jnp.where(lane == sub, own, 0.0), axis=0, keepdims=True)[:, :pairs]
        total = jnp.sum(lse_query, axis=1, keepdims=True) + jnp.sum(every[:, 2, :], axis=0, keepdims=True)[:, :1]
        lm_ref[...] = total / (2 * queries)

    for step in range(1, group):
        share(step).wait_send()


def solution(mesh):
    group = mesh.shape['data']
    batch_spec = P(('replica', 'data'))

    def local_loss(q_hidden, d_hidden, w_proj, q_mask, d_mask, temperature):
        pairs, q_len, hidden = q_hidden.shape
        d_len = d_hidden.shape[1]
        dim = w_proj.shape[1]
        block = pairs * q_len
        chips = group // CORES
        vmem = pl.BlockSpec(memory_space=pltpu.VMEM)
        hbm = pl.BlockSpec(memory_space=pl.ANY)
        out = pl.pallas_call(
            functools.partial(kernel, group),
            out_shape=[jax.ShapeDtypeStruct((1, pairs), jnp.float32), jax.ShapeDtypeStruct((1, pairs), jnp.float32),
                       jax.ShapeDtypeStruct((1, 1), jnp.float32)],
            in_specs=[pl.BlockSpec(memory_space=pltpu.SMEM), hbm, hbm, hbm, hbm, hbm],
            out_specs=[vmem, vmem, vmem],
            scratch_shapes=[
                pltpu.VMEM((block, hidden), jnp.bfloat16),
                pltpu.VMEM((pairs * d_len, hidden), jnp.bfloat16),
                pltpu.VMEM((hidden, dim), jnp.bfloat16),
                pltpu.VMEM((pairs, q_len), jnp.int32),
                pltpu.VMEM((pairs, d_len), jnp.int32),
                pltpu.VMEM((group * block, dim), jnp.bfloat16),
                pltpu.VMEM((pairs * d_len, dim), jnp.bfloat16),
                pltpu.VMEM((pairs * d_len, dim), jnp.bfloat16),
                pltpu.VMEM((pairs, group * block), jnp.float32),
                pltpu.VMEM((group, 4, group * pairs), jnp.float32),
                pltpu.SemaphoreType.DMA,
                pltpu.SemaphoreType.DMA,
                pltpu.SemaphoreType.DMA,
                pltpu.SemaphoreType.DMA,
                pltpu.SemaphoreType.DMA((pairs * d_len // ROWS,)),
                pltpu.SemaphoreType.DMA((chips,)),
                pltpu.SemaphoreType.DMA((group,)),
                pltpu.SemaphoreType.DMA((chips,)),
                pltpu.SemaphoreType.DMA((group - 1,)),
                pltpu.SemaphoreType.DMA((group - 1,)),
            ],
            compiler_params=pltpu.CompilerParams(collective_id=0, has_side_effects=True, vmem_limit_bytes=56 * 2 ** 20),
            name='late_interaction',
        )(temperature.reshape(1), q_hidden.transpose(1, 0, 2).reshape(block, hidden), d_hidden.reshape(pairs * d_len, hidden), w_proj, q_mask, d_mask)
        return out[0].reshape(pairs), out[1].reshape(pairs), out[2].reshape(1)

    return jax.shard_map(local_loss, mesh=mesh, in_specs=(batch_spec, batch_spec, P(), batch_spec, batch_spec, P()),
                         out_specs=(batch_spec, batch_spec, P('replica')), check_vma=False)
```

time: 66.5 us -> 39.1 us (0.59)
  Pallas kernels: 59 us -> 33.6 us
  local copies, waits for them, and re-layouts: 4.34 us -> 2.25 us
    pallas_call x1, Pallas kernels: 59 us -> 33.6 us  [local_loss(): pl.pallas_call(functools.partial(kernel, group), out_shape=[jax.ShapeDtyp...]
    unnamed x3 -> x2, local copies, waits for them, and re-layouts: 4.34 us -> 2.25 us
where the time goes in v2:
time: 39.1 us; the launch traced here: 38.9 us
  Pallas kernels  33.6 us (86%)
  between operations  3.05 us (8%)
  local copies, waits for them, and re-layouts  2.25 us (6%)
    pallas_call x1, Pallas kernels, local_loss(): pl.pallas_call(functools.partial(kernel, group), out_shape=[jax.ShapeDtyp...  33.6 us
    unnamed x2, local copies, waits for them, and re-layouts  2.25 us

profile of v2, /device:TPU:21, one launch (start us, length us, event | category | flops | bytes accessed | tf_op | source)
XLA Modules:
  0.0 38.9 jit_solution(4791101010474437845)
XLA Ops:
  1.3 33.6 %late_interaction.1 = (f32[1,8]{1,0:T(1,128)}, f32[1,8]{1,0:T(1,128)}, f32[1,1]{1,0:T(1,128)}) custom-call(f32[1]{0:T(128)} %bitcast.8.temp_ref, bf16[160,1536]{1,0:T(8,128)(2,1)} %bitcast.10, bf16[6144,1536]{1,0:T(8,128)(2,1)} %bitcast.9, bf16[1536,128]{1,0:T(8,128)(2,1)} %w_hbm.1, s32[8,20]{1,0:T(8,128)} %qm_hbm.1, s32[8,768]{1,0:T(8,128)} %dm_hbm.1), custom_call_target="tpu_custom_call" | custom-call | tf_op jit(solution)/shard_map/late_interaction/pallas_call | solution.py:253
  34.9 1.1 %copy.13 = f32[8]{0:T(128)} copy(f32[8]{0:T(128)} %bitcast.12) | data formatting | bytes 64
  36.0 1.1 %copy.14 = f32[8]{0:T(128)} copy(f32[8]{0:T(128)} %bitcast.11) | data formatting | bytes 64

commit v3 on v2

--- a/solution.py
+++ b/solution.py
@@ -12,9 +12,13 @@
 ROWS = 256
 COLS = 256
 BIG = 2.0 ** 100
-EARLY = 2
+EARLY = 3
 GREET = 2
-STEP = 2
+GROUPS = (2,3,3,4,4,4,2,2)
+LOOK = False
+RELAY = 6
+FENCES = (0, 2, 4, 6, 8, 9)
+DOCS = 1
 LEAD = 2
 
 
@@ -31,8 +35,8 @@
     return raw * lax.rsqrt(jnp.sum(raw * raw, axis=-1, keepdims=True))
 
 
-def kernel(group, temp_ref, q_hbm, d_hbm, w_hbm, qm_hbm, dm_hbm, lq_ref, ld_ref, lm_ref,
-           q_in, d_in, w_in, qm_ref, dm_ref, q_buf, p_buf, bias, best, fin,
+def kernel(group, temp_ref, q_hbm, d_hbm, w_hbm, qm_hbm, dm_hbm, out_ref,
+           q_in, d_in, w_in, qm_ref, dm_ref, q_buf, p_buf, bias, dm_cols, best, grid, fin,
            q_sem, w_sem, qm_sem, dm_sem, d_sem, q_send, q_recv, relay_send, fin_send, fin_recv):
     pairs, q_len = qm_ref.shape
     hidden = q_in.shape[1]
@@ -45,6 +49,7 @@
     queries = group * pairs
     doc_rows = pairs * d_len
     tiles = doc_rows // ROWS
+    depth = hidden // COLS
 
     me = lax.axis_index('data')
     chip = lax.div(me, CORES)
@@ -63,7 +68,7 @@
         rows = pl.ds(i * ROWS, ROWS)
         return pltpu.make_async_copy(d_hbm.at[rows], d_in.at[rows], d_sem.at[i])
 
-    for copy in (qm_copy, w_copy, q_copy, dm_copy):
+    for copy in (w_copy, q_copy, qm_copy, dm_copy):
         copy.start()
     for i in range(EARLY):
         d_copy(i).start()
@@ -72,26 +77,18 @@
     for step in range(1, group):
         pl.semaphore_signal(barrier, inc=1, device_id={'data': lax.rem(me + step, group)}, device_id_type=MESH)
 
-    with jax.named_scope('qmask'):
-        qm_copy.wait()
-        row_pair = lax.broadcasted_iota(jnp.int32, (block, pairs), 0) % pairs
-        picks = (row_pair == lax.broadcasted_iota(jnp.int32, (block, pairs), 1)).astype(jnp.bfloat16)
-        spread = jnp.dot(picks, qm_ref[...].astype(jnp.float32).astype(jnp.bfloat16), preferred_element_type=jnp.float32)
-        row_step = lax.broadcasted_iota(jnp.int32, (block, q_len), 0) // pairs
-        own_step = row_step == lax.broadcasted_iota(jnp.int32, (block, q_len), 1)
-        q_keep = jnp.sum(jnp.where(own_step, spread, 0.0), axis=1, keepdims=True)
     with jax.named_scope('qproj'):
         w_copy.wait()
         q_copy.wait()
         for i in range(EARLY, tiles):
             d_copy(i).start()
         q_raw = jnp.dot(q_in[...], w_in[...], preferred_element_type=jnp.float32)
-        q_buf[0:block, :] = jnp.where(q_keep > 0.5, normalise(q_raw), 0.0).astype(jnp.bfloat16)
-
-    def project(i):
-        rows = pl.ds(i * ROWS, ROWS)
-        raw = jnp.dot(d_in[rows, :], w_in[...], preferred_element_type=jnp.float32)
-        p_buf[rows, :] = normalise(raw).astype(jnp.bfloat16)
+        qm_copy.wait()
+        q_vecs = normalise(q_raw)
+        for t in range(q_len):
+            keep = jnp.broadcast_to(qm_ref[:, t:t + 1], (pairs, dim)) == 1
+            grid[t * pairs:(t + 1) * pairs, :] = jnp.where(keep, q_vecs[t * pairs:(t + 1) * pairs, :], 0.0)
+        q_buf[0:block, :] = grid[0:block, :].astype(jnp.bfloat16)
 
     def slot(s):
         return q_buf.at[pl.ds(s * block, block), :]
@@ -125,64 +122,95 @@
         need(2 * k)
         relay(k).start()
 
+    def project(first, rows):
+        raw = jnp.dot(d_in[first:first + rows, :], w_in[...], preferred_element_type=jnp.float32)
+        p_buf[first:first + rows, :] = normalise(raw).astype(jnp.bfloat16)
+
+    def mask(first, rows):
+        for i in range(first, first + rows, ROWS):
+            doc, start = divmod(i, d_len)
+            bias[i:i + ROWS, :] = jnp.broadcast_to(
+                dm_cols[start:start + ROWS, doc:doc + 1], (ROWS, dim)).astype(jnp.bfloat16)
+
     with jax.named_scope('proj'):
-        for i in range(tiles):
-            if i == 1:
-                with jax.named_scope('dmask'):
-                    dm_copy.wait()
-                    doc_bias = jnp.where(dm_ref[...] == 1, 0.0, -BIG)
-                    doc_bias = jnp.concatenate([doc_bias, jnp.zeros((128 - pairs, d_len), jnp.float32)], axis=0)
-                    doc_bias = jnp.transpose(doc_bias)
-                    for j in range(pairs):
-                        bias[j * d_len:(j + 1) * d_len, :] = jnp.broadcast_to(
-                            doc_bias[:, j:j + 1], (d_len, dim)).astype(jnp.bfloat16)
-            if i == GREET:
+        starts = [sum(GROUPS[:g]) for g in range(len(GROUPS) + 1)]
+        for g in range(len(GROUPS)):
+            if g == GREET:
                 with jax.named_scope('barrier'):
                     pl.semaphore_wait(barrier, group - 1)
                 to_partner().start()
                 for k in range(1, chips):
                     to_chip(k).start()
-            if i % STEP == 0:
-                for t in range(i, i + STEP):
-                    d_copy(t).wait()
-            project(i)
-        pass_on(1)
-
+            if g == RELAY:
+                pass_on(1)
+            if LOOK:
+                if g == 0:
+                    for i in range(starts[1]):
+                        d_copy(i).wait()
+                if g + 1 < len(GROUPS):
+                    for i in range(starts[g + 1], starts[g + 2]):
+                        d_copy(i).wait()
+            else:
+                with jax.named_scope(f'dw{g}'):
+                    for i in range(starts[g], starts[g + 1]):
+                        d_copy(i).wait()
+            for i in range(starts[g], starts[g + 1]):
+                project(i * ROWS, ROWS)
+            if g == 0:
+                dm_copy.wait()
+                masked = jnp.where(dm_ref[...] == 1, 0.0, -BIG)
+                masked = jnp.concatenate([masked, jnp.zeros((128 - pairs, d_len), jnp.float32)], axis=0)
+                dm_cols[...] = jnp.transpose(masked)
+            else:
+                mask(starts[g - 1] * ROWS, GROUPS[g - 1] * ROWS)
+        mask(starts[-2] * ROWS, GROUPS[-1] * ROWS)
+
+    ones = (lax.broadcasted_iota(jnp.int32, (COLS, dim), 1) == 0).astype(jnp.bfloat16)
+    score_tiles = tokens // COLS
     first_tile = [s * block // COLS for s in range(group)]
-    ones = (lax.broadcasted_iota(jnp.int32, (COLS, dim), 1) == 0).astype(jnp.bfloat16)
-    for n in range(tokens // COLS):
+    sums = {}
+
+    def fetch(n):
+        after = min([f for f in FENCES if f > n] + [score_tiles])
+        later = min([f for f in FENCES if f > after] + [score_tiles])
+        for s in range(group):
+            if first_tile[s] < after and s % 2 == 0:
+                need(s)
         for k in range(2, chips):
-            if max(first_tile[2 * k + 1] - LEAD, 0) == n:
+            if first_tile[2 * k + 1] < later and k not in passed:
+                passed.add(k)
                 pass_on(k)
         for s in range(group):
-            if first_tile[s] == n:
+            if first_tile[s] < after:
                 need(s)
-        with jax.named_scope(f'score{n}'):
+
+    passed = set()
+
+    def add_up(n):
+        by_token = jnp.transpose(best[n % 2])
+        for row in range(COLS // pairs):
+            s = (n * COLS // pairs + row) // q_len
+            term = by_token[row * pairs:(row + 1) * pairs, :]
+            sums[s] = sums[s] + term if s in sums else term
+        for s in [s for s in sums if (s + 1) * block <= (n + 1) * COLS]:
+            owner = at_offset(offsets[s // 2]) * CORES + (core if s % 2 == 0 else CORES - 1 - core)
+            grid[pl.ds(pl.multiple_of(owner * pairs, pairs), pairs), 0:pairs] = sums.pop(s)
+
+    with jax.named_scope('scores'):
+        for n in range(score_tiles):
+            if n in FENCES:
+                fetch(n)
             rhs = jnp.concatenate([q_buf[n * COLS:(n + 1) * COLS, :], ones], axis=1)
-            for j in range(0, pairs):
-                rows = pl.ds(j * d_len, d_len)
+            for j in range(0, pairs, DOCS):
+                rows = slice(j * d_len, (j + DOCS) * d_len)
                 lhs = jnp.concatenate([p_buf[rows, :], bias[rows, :]], axis=1)
                 sim = lax.dot_general(lhs, rhs, (((1,), (1,)), ((), ())), preferred_element_type=jnp.float32)
-                best[pl.ds(j, 1), n * COLS:(n + 1) * COLS] = jnp.max(sim, axis=0, keepdims=True)
-
-    with jax.named_scope('segsum'):
-        scores = jnp.zeros((pairs, queries), jnp.float32)
-        for n in range(tokens // COLS):
-            row = lax.broadcasted_iota(jnp.int32, (COLS, queries), 0) + n * COLS
-            first, last = n * COLS // block, (COLS * (n + 1) - 1) // block
-            start = None
-            for s in range(first, last + 1):
-                owner = at_offset(offsets[s // 2]) * CORES + (core if s % 2 == 0 else CORES - 1 - core)
-                start = owner * pairs if start is None else jnp.where(row >= s * block, owner * pairs, start)
-            query = row % pairs + start
-            picks = (query == lax.broadcasted_iota(jnp.int32, (COLS, queries), 1)).astype(jnp.bfloat16)
-            part = best[:, n * COLS:(n + 1) * COLS]
-            high = part.astype(jnp.bfloat16)
-            rest = part - high.astype(jnp.float32)
-            mid = rest.astype(jnp.bfloat16)
-            low = (rest - mid.astype(jnp.float32)).astype(jnp.bfloat16)
-            for piece in (low, mid, high):
-                scores += jnp.dot(piece, picks, preferred_element_type=jnp.float32)
+                for i in range(DOCS):
+                    best[n % 2, j + i:j + i + 1, :] = jnp.max(sim[i * d_len:(i + 1) * d_len], axis=0, keepdims=True)
+            if n:
+                add_up(n - 1)
+        add_up(score_tiles - 1)
+    scores = jnp.transpose(grid[0:queries, 0:pairs])
 
     with jax.named_scope('partial'):
         z = scores / temp_ref[0]
@@ -212,7 +240,7 @@
     for step in range(1, group):
         share(step).start()
 
-    ld_ref[...] = jnp.sum(jnp.where(lane == sub, loss_doc, 0.0), axis=0, keepdims=True)[:, :pairs]
+    out_ref[1:2, 0:pairs] = jnp.sum(jnp.where(lane == sub, loss_doc, 0.0), axis=0, keepdims=True)[:, :pairs]
 
     with jax.named_scope('shwait'):
         to_partner().wait_send()
@@ -230,9 +258,9 @@
         loss_query = lse_query - pos_row
         own = jnp.where(lane == me * pairs + sub, loss_query, 0.0)
         own = jnp.sum(own, axis=1, keepdims=True)
-        lq_ref[...] = jnp.sum(jnp.where(lane == sub, own, 0.0), axis=0, keepdims=True)[:, :pairs]
+        out_ref[0:1, 0:pairs] = jnp.sum(jnp.where(lane == sub, own, 0.0), axis=0, keepdims=True)[:, :pairs]
         total = jnp.sum(lse_query, axis=1, keepdims=True) + jnp.sum(every[:, 2, :], axis=0, keepdims=True)[:, :1]
-        lm_ref[...] = total / (2 * queries)
+        out_ref[2:3, 0:1] = total / (2 * queries)
 
     for step in range(1, group):
         share(step).wait_send()
@@ -252,10 +280,9 @@
         hbm = pl.BlockSpec(memory_space=pl.ANY)
         out = pl.pallas_call(
             functools.partial(kernel, group),
-            out_shape=[jax.ShapeDtypeStruct((1, pairs), jnp.float32), jax.ShapeDtypeStruct((1, pairs), jnp.float32),
-                       jax.ShapeDtypeStruct((1, 1), jnp.float32)],
+            out_shape=[jax.ShapeDtypeStruct((8, 128), jnp.float32)],
             in_specs=[pl.BlockSpec(memory_space=pltpu.SMEM), hbm, hbm, hbm, hbm, hbm],
-            out_specs=[vmem, vmem, vmem],
+            out_specs=[vmem],
             scratch_shapes=[
                 pltpu.VMEM((block, hidden), jnp.bfloat16),
                 pltpu.VMEM((pairs * d_len, hidden), jnp.bfloat16),
@@ -265,7 +292,9 @@
                 pltpu.VMEM((group * block, dim), jnp.bfloat16),
                 pltpu.VMEM((pairs * d_len, dim), jnp.bfloat16),
                 pltpu.VMEM((pairs * d_len, dim), jnp.bfloat16),
-                pltpu.VMEM((pairs, group * block), jnp.float32),
+                pltpu.VMEM((d_len, 128), jnp.float32),
+                pltpu.VMEM((2, pairs, COLS), jnp.float32),
+                pltpu.VMEM((max(block, group * pairs), dim), jnp.float32),
                 pltpu.VMEM((group, 4, group * pairs), jnp.float32),
                 pltpu.SemaphoreType.DMA,
                 pltpu.SemaphoreType.DMA,
@@ -281,7 +310,14 @@
             compiler_params=pltpu.CompilerParams(collective_id=0, has_side_effects=True, vmem_limit_bytes=56 * 2 ** 20),
             name='late_interaction',
         )(temperature.reshape(1), q_hidden.transpose(1, 0, 2).reshape(block, hidden), d_hidden.reshape(pairs * d_len, hidden), w_proj, q_mask, d_mask)
-        return out[0].reshape(pairs), out[1].reshape(pairs), out[2].reshape(1)
+        packed = out[0]
+        def unpack(x_ref, q_ref, d_ref, m_ref):
+            q_ref[...] = x_ref[0:1, 0:pairs]
+            d_ref[...] = x_ref[1:2, 0:pairs]
+            m_ref[...] = x_ref[2:3, 0:1]
+        res = pl.pallas_call(unpack, out_shape=[jax.ShapeDtypeStruct((1, pairs), jnp.float32), jax.ShapeDtypeStruct((1, pairs), jnp.float32),
+                       jax.ShapeDtypeStruct((1, 1), jnp.float32)], in_specs=[vmem], out_specs=[vmem, vmem, vmem], name='unpack')(packed)
+        return res[0].reshape(pairs), res[1].reshape(pairs), res[2].reshape(1)
 
     return jax.shard_map(local_loss, mesh=mesh, in_specs=(batch_spec, batch_spec, P(), batch_spec, batch_spec, P()),
                          out_specs=(batch_spec, batch_spec, P('replica')), check_vma=False)

time: 39.1 us -> 34.9 us (0.89)
  local copies, waits for them, and re-layouts: 2.25 us -> 0 us
  between operations: 3.05 us -> 1.29 us
    unnamed x2 -> x0, local copies, waits for them, and re-layouts: 2.25 us -> none
    pallas_call x1, Pallas kernels: 33.6 us -> 32.3 us  [local_loss(): pl.pallas_call(functools.partial(kernel, group), out_shape=[jax.ShapeDtyp...]
    pallas_call x0 -> x1, Pallas kernels: none -> 1.19 us  [local_loss(): pl.pallas_call(unpack, out_shape=[jax.ShapeDtypeStruct((1, pairs), jnp.fl...]
where the time goes in v3:
time: 34.9 us; the launch traced here: 34.8 us
  Pallas kernels  33.5 us (96%)
  between operations  1.29 us (4%)
    pallas_call x1, Pallas kernels, local_loss(): pl.pallas_call(functools.partial(kernel, group), out_shape=[jax.ShapeDtyp...  32.3 us
    pallas_call x1, Pallas kernels, local_loss(): pl.pallas_call(unpack, out_shape=[jax.ShapeDtypeStruct((1, pairs), jnp.fl...  1.19 us

profile of v3, /device:TPU:21, one launch (start us, length us, event | category | flops | bytes accessed | tf_op | source)
XLA Modules:
  0.0 34.8 jit_solution(14751360840370818722)
XLA Ops:
  1.3 32.3 %late_interaction.1.x_ref = f32[8,128]{1,0:T(8,128)} custom-call(f32[1]{0:T(128)} %bitcast.8.temp_ref, bf16[160,1536]{1,0:T(8,128)(2,1)} %bitcast.10, bf16[6144,1536]{1,0:T(8,128)(2,1)} %bitcast.9, bf16[1536,128]{1,0:T(8,128)(2,1)} %w_hbm.1, s32[8,20]{1,0:T(8,128)} %qm_hbm.1, s32[8,768]{1,0:T(8,128)} %dm_hbm.1), custom_call_target="tpu_custom_call" | custom-call | tf_op jit(solution)/shard_map/late_interaction/pallas_call | solution.py:281
  33.6 1.2 %unpack.1 = (f32[1,8]{1,0:T(1,128)}, f32[1,8]{1,0:T(1,128)}, f32[1,1]{1,0:T(1,128)}) custom-call(f32[8,128]{1,0:T(8,128)} %late_interaction.1.x_ref), custom_call_target="tpu_custom_call" | custom-call | tf_op jit(solution)/shard_map/unpack/pallas_call | solution.py:318

commit v4 on v3

--- a/solution.py
+++ b/solution.py
@@ -13,13 +13,13 @@
 COLS = 256
 BIG = 2.0 ** 100
 EARLY = 3
-GREET = 2
-GROUPS = (2,3,3,4,4,4,2,2)
-LOOK = False
-RELAY = 6
-FENCES = (0, 2, 4, 6, 8, 9)
-DOCS = 1
-LEAD = 2
+ISSUED = (12,12,18,24,24,24)
+DOCS = (1, 1, 2, 2, 2)
+SENDS = (0, 0, 1, 2)
+GREET_HIGH = 1
+GREET_LOW = 2
+HOME = 4
+FENCES = (1,2,4,6,8)
 
 
 def chip_offsets(chips):
@@ -31,13 +31,23 @@
     return order
 
 
+def slot_order(chips):
+    direct, relayed = [0], [1]
+    for first in range(1, chips, 2):
+        count = min(2, chips - first)
+        base = 2 * first
+        direct += [base + i for i in range(count)]
+        relayed += [base + count + i for i in range(count)]
+    return direct, relayed
+
+
 def normalise(raw):
     return raw * lax.rsqrt(jnp.sum(raw * raw, axis=-1, keepdims=True))
 
 
-def kernel(group, temp_ref, q_hbm, d_hbm, w_hbm, qm_hbm, dm_hbm, out_ref,
-           q_in, d_in, w_in, qm_ref, dm_ref, q_buf, p_buf, bias, dm_cols, best, grid, fin,
-           q_sem, w_sem, qm_sem, dm_sem, d_sem, q_send, q_recv, relay_send, fin_send, fin_recv):
+def kernel(group, temp_hbm, q_hbm, d_hbm, w_hbm, qm_hbm, dm_hbm, out_ref,
+           temp_ref, q_in, d_in, w_in, qm_ref, dm_ref, q_buf, p_buf, bias, dm_cols, best, grid, fin,
+           temp_sem, q_sem, w_sem, qm_sem, dm_sem, d_sem, q_send, q_recv, relay_send, fin_send, fin_recv):
     pairs, q_len = qm_ref.shape
     hidden = q_in.shape[1]
     d_len = dm_ref.shape[1]
@@ -45,6 +55,7 @@
     block = pairs * q_len
     chips = group // CORES
     offsets = chip_offsets(chips)
+    direct, relayed = slot_order(chips)
     tokens = group * block
     queries = group * pairs
     doc_rows = pairs * d_len
@@ -63,6 +74,7 @@
     q_copy = pltpu.make_async_copy(q_hbm, q_in, q_sem)
     qm_copy = pltpu.make_async_copy(qm_hbm, qm_ref, qm_sem)
     dm_copy = pltpu.make_async_copy(dm_hbm, dm_ref, dm_sem)
+    temp_copy = pltpu.make_async_copy(temp_hbm, temp_ref, temp_sem)
 
     def d_copy(i):
         rows = pl.ds(i * ROWS, ROWS)
@@ -72,24 +84,12 @@
         copy.start()
     for i in range(EARLY):
         d_copy(i).start()
+    temp_copy.start()
 
     barrier = pltpu.get_barrier_semaphore()
     for step in range(1, group):
         pl.semaphore_signal(barrier, inc=1, device_id={'data': lax.rem(me + step, group)}, device_id_type=MESH)
 
-    with jax.named_scope('qproj'):
-        w_copy.wait()
-        q_copy.wait()
-        for i in range(EARLY, tiles):
-            d_copy(i).start()
-        q_raw = jnp.dot(q_in[...], w_in[...], preferred_element_type=jnp.float32)
-        qm_copy.wait()
-        q_vecs = normalise(q_raw)
-        for t in range(q_len):
-            keep = jnp.broadcast_to(qm_ref[:, t:t + 1], (pairs, dim)) == 1
-            grid[t * pairs:(t + 1) * pairs, :] = jnp.where(keep, q_vecs[t * pairs:(t + 1) * pairs, :], 0.0)
-        q_buf[0:block, :] = grid[0:block, :].astype(jnp.bfloat16)
-
     def slot(s):
         return q_buf.at[pl.ds(s * block, block), :]
 
@@ -99,11 +99,12 @@
 
     def to_chip(k):
         back = offsets.index(-offsets[k]) if -offsets[k] in offsets else k
-        return pltpu.make_async_remote_copy(slot(0), slot(2 * back), q_send.at[k], q_recv.at[2 * back],
+        place = direct[back]
+        return pltpu.make_async_remote_copy(slot(0), slot(place), q_send.at[k], q_recv.at[place],
                                             device_id={'data': at_offset(offsets[k]) * CORES + core}, device_id_type=MESH)
 
     def relay(k):
-        return pltpu.make_async_remote_copy(slot(2 * k), slot(2 * k + 1), relay_send.at[k], q_recv.at[2 * k + 1],
+        return pltpu.make_async_remote_copy(slot(direct[k]), slot(relayed[k]), relay_send.at[k], q_recv.at[relayed[k]],
                                             device_id={'data': partner}, device_id_type=MESH)
 
     def arrival(s):
@@ -119,65 +120,102 @@
             arrived.add(s)
 
     def pass_on(k):
-        need(2 * k)
+        need(direct[k])
         relay(k).start()
 
-    def project(first, rows):
-        raw = jnp.dot(d_in[first:first + rows, :], w_in[...], preferred_element_type=jnp.float32)
-        p_buf[first:first + rows, :] = normalise(raw).astype(jnp.bfloat16)
-
-    def mask(first, rows):
-        for i in range(first, first + rows, ROWS):
-            doc, start = divmod(i, d_len)
-            bias[i:i + ROWS, :] = jnp.broadcast_to(
-                dm_cols[start:start + ROWS, doc:doc + 1], (ROWS, dim)).astype(jnp.bfloat16)
-
-    with jax.named_scope('proj'):
-        starts = [sum(GROUPS[:g]) for g in range(len(GROUPS) + 1)]
-        for g in range(len(GROUPS)):
-            if g == GREET:
-                with jax.named_scope('barrier'):
-                    pl.semaphore_wait(barrier, group - 1)
-                to_partner().start()
-                for k in range(1, chips):
-                    to_chip(k).start()
-            if g == RELAY:
-                pass_on(1)
-            if LOOK:
-                if g == 0:
-                    for i in range(starts[1]):
-                        d_copy(i).wait()
-                if g + 1 < len(GROUPS):
-                    for i in range(starts[g + 1], starts[g + 2]):
-                        d_copy(i).wait()
-            else:
-                with jax.named_scope(f'dw{g}'):
-                    for i in range(starts[g], starts[g + 1]):
-                        d_copy(i).wait()
-            for i in range(starts[g], starts[g + 1]):
-                project(i * ROWS, ROWS)
-            if g == 0:
-                dm_copy.wait()
-                masked = jnp.where(dm_ref[...] == 1, 0.0, -BIG)
-                masked = jnp.concatenate([masked, jnp.zeros((128 - pairs, d_len), jnp.float32)], axis=0)
-                dm_cols[...] = jnp.transpose(masked)
-            else:
-                mask(starts[g - 1] * ROWS, GROUPS[g - 1] * ROWS)
-        mask(starts[-2] * ROWS, GROUPS[-1] * ROWS)
-
-    ones = (lax.broadcasted_iota(jnp.int32, (COLS, dim), 1) == 0).astype(jnp.bfloat16)
     score_tiles = tokens // COLS
     first_tile = [s * block // COLS for s in range(group)]
+    ones = (lax.broadcasted_iota(jnp.int32, (COLS, dim), 1) == 0).astype(jnp.bfloat16)
+
+    def project_queries():
+        q_vecs = normalise(jnp.dot(q_in[...], w_in[...], preferred_element_type=jnp.float32))
+        for t in range(q_len):
+            keep = jnp.broadcast_to(qm_ref[:, t:t + 1], (pairs, dim)) == 1
+            grid[t * pairs:(t + 1) * pairs, :] = jnp.where(keep, q_vecs[t * pairs:(t + 1) * pairs, :], 0.0)
+        q_buf[0:block, :] = grid[0:block, :].astype(jnp.bfloat16)
+
+    def project(doc):
+        for first in range(doc * d_len, (doc + 1) * d_len, ROWS):
+            raw = jnp.dot(d_in[first:first + ROWS, :], w_in[...], preferred_element_type=jnp.float32)
+            p_buf[first:first + ROWS, :] = normalise(raw).astype(jnp.bfloat16)
+
+    def turn_masks():
+        masked = jnp.where(dm_ref[...] == 1, 0.0, -BIG)
+        masked = jnp.concatenate([masked, jnp.zeros((128 - pairs, d_len), jnp.float32)], axis=0)
+        dm_cols[...] = jnp.transpose(masked)
+
+    def mask(doc):
+        bias[doc * d_len:(doc + 1) * d_len, :] = jnp.broadcast_to(
+            dm_cols[:, doc:doc + 1], (d_len, dim)).astype(jnp.bfloat16)
+
+    def score(n, docs):
+        rhs = jnp.concatenate([q_buf[n * COLS:(n + 1) * COLS, :], ones], axis=1)
+        for doc in docs:
+            rows = slice(doc * d_len, (doc + 1) * d_len)
+            lhs = jnp.concatenate([p_buf[rows, :], bias[rows, :]], axis=1)
+            sim = lax.dot_general(lhs, rhs, (((1,), (1,)), ((), ())), preferred_element_type=jnp.float32)
+            best[n % 2, doc:doc + 1, :] = jnp.max(sim, axis=0, keepdims=True)
+
+    def send_later(turn):
+        for k in range(1, chips):
+            if SENDS[abs(offsets[k]) - 1] == turn:
+                to_chip(k).start()
+
+    def send_queries():
+        with jax.named_scope('barrier'):
+            pl.semaphore_wait(barrier, group - 1)
+        to_partner().start()
+        send_later(0)
+
+    done = scored = 0
+    with jax.named_scope('proj'):
+        for step, count in enumerate(DOCS):
+            if step == GREET_HIGH:
+                pl.when(chip >= chips // 2)(send_queries)
+            if step == GREET_LOW:
+                pl.when(chip < chips // 2)(send_queries)
+            for turn in range(1, max(SENDS) + 1):
+                if step == GREET_HIGH + turn:
+                    pl.when(chip >= chips // 2)(functools.partial(send_later, turn))
+                if step == GREET_LOW + turn:
+                    pl.when(chip < chips // 2)(functools.partial(send_later, turn))
+            if step == HOME:
+                need(1)
+            if step == 0:
+                with jax.named_scope('dmaw'):
+                    w_copy.wait()
+                    q_copy.wait()
+                    for i in range(EARLY, ISSUED[0]):
+                        d_copy(i).start()
+                    qm_copy.wait()
+                    dm_copy.wait()
+            for i in range(ISSUED[step], ISSUED[step + 1]):
+                d_copy(i).start()
+            with jax.named_scope(f'dw{step}'):
+                for i in range(done * d_len // ROWS, (done + count) * d_len // ROWS):
+                    d_copy(i).wait()
+            if step == 0:
+                project_queries()
+                turn_masks()
+            for doc in range(done, done + count):
+                project(doc)
+            if step >= HOME:
+                score(0, range(scored, done))
+                scored = done
+            for doc in range(done, done + count):
+                mask(doc)
+            done += count
+
     sums = {}
 
     def fetch(n):
         after = min([f for f in FENCES if f > n] + [score_tiles])
         later = min([f for f in FENCES if f > after] + [score_tiles])
         for s in range(group):
-            if first_tile[s] < after and s % 2 == 0:
+            if first_tile[s] < after and s in direct:
                 need(s)
-        for k in range(2, chips):
-            if first_tile[2 * k + 1] < later and k not in passed:
+        for k in range(1, chips):
+            if first_tile[relayed[k]] < later and k not in passed:
                 passed.add(k)
                 pass_on(k)
         for s in range(group):
@@ -193,26 +231,23 @@
             term = by_token[row * pairs:(row + 1) * pairs, :]
             sums[s] = sums[s] + term if s in sums else term
         for s in [s for s in sums if (s + 1) * block <= (n + 1) * COLS]:
-            owner = at_offset(offsets[s // 2]) * CORES + (core if s % 2 == 0 else CORES - 1 - core)
+            place = direct if s in direct else relayed
+            owner = at_offset(offsets[place.index(s)]) * CORES + (core if s in direct else CORES - 1 - core)
             grid[pl.ds(pl.multiple_of(owner * pairs, pairs), pairs), 0:pairs] = sums.pop(s)
 
     with jax.named_scope('scores'):
-        for n in range(score_tiles):
+        for n in range(1, score_tiles):
             if n in FENCES:
                 fetch(n)
-            rhs = jnp.concatenate([q_buf[n * COLS:(n + 1) * COLS, :], ones], axis=1)
-            for j in range(0, pairs, DOCS):
-                rows = slice(j * d_len, (j + DOCS) * d_len)
-                lhs = jnp.concatenate([p_buf[rows, :], bias[rows, :]], axis=1)
-                sim = lax.dot_general(lhs, rhs, (((1,), (1,)), ((), ())), preferred_element_type=jnp.float32)
-                for i in range(DOCS):
-                    best[n % 2, j + i:j + i + 1, :] = jnp.max(sim[i * d_len:(i + 1) * d_len], axis=0, keepdims=True)
-            if n:
-                add_up(n - 1)
+            if n == 1:
+                score(0, range(scored, pairs))
+            score(n, range(pairs))
+            add_up(n - 1)
         add_up(score_tiles - 1)
     scores = jnp.transpose(grid[0:queries, 0:pairs])
 
     with jax.named_scope('partial'):
+        temp_copy.wait()
         z = scores / temp_ref[0]
         lane = lax.broadcasted_iota(jnp.int32, (pairs, queries), 1)
         sub = lax.broadcasted_iota(jnp.int32, (pairs, queries), 0)
@@ -237,7 +272,7 @@
         return pltpu.make_async_remote_copy(fin.at[source], fin.at[source], fin_send.at[step - 1], fin_recv.at[step - 1],
                                             device_id={'data': source}, device_id_type=MESH)
 
-    for step in range(1, group):
+    for step in sorted(range(1, group), key=lambda step: abs(2 * step - group)):
         share(step).start()
 
     out_ref[1:2, 0:pairs] = jnp.sum(jnp.where(lane == sub, loss_doc, 0.0), axis=0, keepdims=True)[:, :pairs]
@@ -281,9 +316,10 @@
         out = pl.pallas_call(
             functools.partial(kernel, group),
             out_shape=[jax.ShapeDtypeStruct((8, 128), jnp.float32)],
-            in_specs=[pl.BlockSpec(memory_space=pltpu.SMEM), hbm, hbm, hbm, hbm, hbm],
+            in_specs=[hbm, hbm, hbm, hbm, hbm, hbm],
             out_specs=[vmem],
             scratch_shapes=[
+                pltpu.SMEM((1,), jnp.float32),
                 pltpu.VMEM((block, hidden), jnp.bfloat16),
                 pltpu.VMEM((pairs * d_len, hidden), jnp.bfloat16),
                 pltpu.VMEM((hidden, dim), jnp.bfloat16),
@@ -296,6 +332,7 @@
                 pltpu.VMEM((2, pairs, COLS), jnp.float32),
                 pltpu.VMEM((max(block, group * pairs), dim), jnp.float32),
                 pltpu.VMEM((group, 4, group * pairs), jnp.float32),
+                pltpu.SemaphoreType.DMA,
                 pltpu.SemaphoreType.DMA,
                 pltpu.SemaphoreType.DMA,
                 pltpu.SemaphoreType.DMA,

time: 34.9 us -> 33.9 us (0.971)
  Pallas kernels: 33.5 us -> 32.5 us
    pallas_call x1, Pallas kernels: 32.3 us -> 31.3 us  [local_loss(): pl.pallas_call(functools.partial(kernel, group), out_shape=[jax.ShapeDtyp...]
where the time goes in v4:
time: 33.9 us; the launch traced here: 33.8 us
  Pallas kernels  32.5 us (96%)
  between operations  1.29 us (4%)
    pallas_call x1, Pallas kernels, local_loss(): pl.pallas_call(functools.partial(kernel, group), out_shape=[jax.ShapeDtyp...  31.3 us
    pallas_call x1, Pallas kernels, local_loss(): pl.pallas_call(unpack, out_shape=[jax.ShapeDtypeStruct((1, pairs), jnp.fl...  1.19 us

profile of v4, /device:TPU:21, one launch (start us, length us, event | category | flops | bytes accessed | tf_op | source)
XLA Modules:
  0.0 33.8 jit_solution(11867247733093606899)
XLA Ops:
  1.3 31.3 %late_interaction.1.x_ref = f32[8,128]{1,0:T(8,128)} custom-call(f32[1]{0:T(128)} %bitcast.8.temp_hbm, bf16[160,1536]{1,0:T(8,128)(2,1)} %bitcast.10, bf16[6144,1536]{1,0:T(8,128)(2,1)} %bitcast.9, bf16[1536,128]{1,0:T(8,128)(2,1)} %w_hbm.1, s32[8,20]{1,0:T(8,128)} %qm_hbm.1, s32[8,768]{1,0:T(8,128)} %dm_hbm.1), custom_call_target="tpu_custom_call" | custom-call | tf_op jit(solution)/shard_map/late_interaction/pallas_call | solution.py:316
  32.6 1.2 %unpack.1 = (f32[1,8]{1,0:T(1,128)}, f32[1,8]{1,0:T(1,128)}, f32[1,1]{1,0:T(1,128)}) custom-call(f32[8,128]{1,0:T(8,128)} %late_interaction.1.x_ref), custom_call_target="tpu_custom_call" | custom-call | tf_op jit(solution)/shard_map/unpack/pallas_call | solution.py:355

commit v5 on v4

--- a/solution.py
+++ b/solution.py
@@ -12,6 +12,9 @@
 ROWS = 256
 COLS = 256
 BIG = 2.0 ** 100
+VMEM = 56552448
+APART = True
+SOON = 6
 EARLY = 3
 ISSUED = (12,12,18,24,24,24)
 DOCS = (1, 1, 2, 2, 2)
@@ -184,17 +187,22 @@
             if step == 0:
                 with jax.named_scope('dmaw'):
                     w_copy.wait()
+                    for i in range(EARLY, SOON):
+                        d_copy(i).start()
                     q_copy.wait()
-                    for i in range(EARLY, ISSUED[0]):
+                    for i in range(SOON, ISSUED[0]):
                         d_copy(i).start()
                     qm_copy.wait()
                     dm_copy.wait()
+                    if APART:
+                        project_queries()
+                        turn_masks()
             for i in range(ISSUED[step], ISSUED[step + 1]):
                 d_copy(i).start()
             with jax.named_scope(f'dw{step}'):
                 for i in range(done * d_len // ROWS, (done + count) * d_len // ROWS):
                     d_copy(i).wait()
-            if step == 0:
+            if step == 0 and not APART:
                 project_queries()
                 turn_masks()
             for doc in range(done, done + count):
@@ -312,7 +320,7 @@
         block = pairs * q_len
         chips = group // CORES
         vmem = pl.BlockSpec(memory_space=pltpu.VMEM)
-        hbm = pl.BlockSpec(memory_space=pl.ANY)
+        hbm = pl.BlockSpec(memory_space=pltpu.HBM)
         out = pl.pallas_call(
             functools.partial(kernel, group),
             out_shape=[jax.ShapeDtypeStruct((8, 128), jnp.float32)],
@@ -344,7 +352,7 @@
                 pltpu.SemaphoreType.DMA((group - 1,)),
                 pltpu.SemaphoreType.DMA((group - 1,)),
             ],
-            compiler_params=pltpu.CompilerParams(collective_id=0, has_side_effects=True, vmem_limit_bytes=56 * 2 ** 20),
+            compiler_params=pltpu.CompilerParams(collective_id=0, has_side_effects=True, vmem_limit_bytes=VMEM),
             name='late_interaction',
         )(temperature.reshape(1), q_hidden.transpose(1, 0, 2).reshape(block, hidden), d_hidden.reshape(pairs * d_len, hidden), w_proj, q_mask, d_mask)
         packed = out[0]
@@ -353,7 +361,8 @@
             d_ref[...] = x_ref[1:2, 0:pairs]
             m_ref[...] = x_ref[2:3, 0:1]
         res = pl.pallas_call(unpack, out_shape=[jax.ShapeDtypeStruct((1, pairs), jnp.float32), jax.ShapeDtypeStruct((1, pairs), jnp.float32),
-                       jax.ShapeDtypeStruct((1, 1), jnp.float32)], in_specs=[vmem], out_specs=[vmem, vmem, vmem], name='unpack')(packed)
+                       jax.ShapeDtypeStruct((1, 1), jnp.float32)], in_specs=[vmem], out_specs=[vmem, vmem, vmem],
+                       compiler_params=pltpu.CompilerParams(vmem_limit_bytes=2 ** 20), name='unpack')(packed)
         return res[0].reshape(pairs), res[1].reshape(pairs), res[2].reshape(1)
 
     return jax.shard_map(local_loss, mesh=mesh, in_specs=(batch_spec, batch_spec, P(), batch_spec, batch_spec, P()),

time: 33.9 us -> 32.6 us (0.962)
  Pallas kernels: 32.5 us -> 31.2 us
    pallas_call x1, Pallas kernels: 1.19 us -> 0.52 us  [local_loss(): pl.pallas_call(unpack, out_shape=[jax.ShapeDtypeStruct((1, pairs), jnp.fl...]
    pallas_call x1, Pallas kernels: 31.3 us -> 30.7 us  [local_loss(): pl.pallas_call(functools.partial(kernel, group), out_shape=[jax.ShapeDtyp...]
where the time goes in v5:
time: 32.6 us; the launch traced here: 32.5 us
  Pallas kernels  31.2 us (96%)
  between operations  1.29 us (4%)
    pallas_call x1, Pallas kernels, local_loss(): pl.pallas_call(functools.partial(kernel, group), out_shape=[jax.ShapeDtyp...  30.7 us

profile of v5, /device:TPU:21, one launch (start us, length us, event | category | flops | bytes accessed | tf_op | source)
XLA Modules:
  0.0 32.5 jit_solution(5668588846512060266)
XLA Ops:
  1.3 30.7 %late_interaction.1.x_ref = f32[8,128]{1,0:T(8,128)S(1)} custom-call(f32[1]{0:T(128)} %bitcast.8.temp_hbm, bf16[160,1536]{1,0:T(8,128)(2,1)} %bitcast.10, bf16[6144,1536]{1,0:T(8,128)(2,1)} %bitcast.9, bf16[1536,128]{1,0:T(8,128)(2,1)} %w_hbm.1, s32[8,20]{1,0:T(8,128)} %qm_hbm.1, s32[8,768]{1,0:T(8,128)} %dm_hbm.1), custom_call_target="tpu_custom_call" | custom-call | tf_op jit(solution)/shard_map/late_interaction/pallas_call | solution.py:324
  32.0 0.5 %unpack.1 = (f32[1,8]{1,0:T(1,128)}, f32[1,8]{1,0:T(1,128)}, f32[1,1]{1,0:T(1,128)}) custom-call(f32[8,128]{1,0:T(8,128)S(1)} %late_interaction.1.x_ref), custom_call_target="tpu_custom_call" | custom-call | tf_op jit(solution)/shard_map/unpack/pallas_call | solution.py:363

commit v6 on v5

--- a/solution.py
+++ b/solution.py
@@ -140,16 +140,15 @@
     def project(doc):
         for first in range(doc * d_len, (doc + 1) * d_len, ROWS):
             raw = jnp.dot(d_in[first:first + ROWS, :], w_in[...], preferred_element_type=jnp.float32)
-            p_buf[first:first + ROWS, :] = normalise(raw).astype(jnp.bfloat16)
+            part = first - doc * d_len
+            masked = jnp.broadcast_to(dm_cols[part:part + ROWS, doc:doc + 1], (ROWS, dim))
+            p_buf[first:first + ROWS, :] = jnp.where(masked == 0.0, normalise(raw), 0.0).astype(jnp.bfloat16)
+            bias[first:first + ROWS, :] = masked.astype(jnp.bfloat16)
 
     def turn_masks():
         masked = jnp.where(dm_ref[...] == 1, 0.0, -BIG)
         masked = jnp.concatenate([masked, jnp.zeros((128 - pairs, d_len), jnp.float32)], axis=0)
         dm_cols[...] = jnp.transpose(masked)
-
-    def mask(doc):
-        bias[doc * d_len:(doc + 1) * d_len, :] = jnp.broadcast_to(
-            dm_cols[:, doc:doc + 1], (d_len, dim)).astype(jnp.bfloat16)
 
     def score(n, docs):
         rhs = jnp.concatenate([q_buf[n * COLS:(n + 1) * COLS, :], ones], axis=1)
@@ -210,8 +209,6 @@
             if step >= HOME:
                 score(0, range(scored, done))
                 scored = done
-            for doc in range(done, done + count):
-                mask(doc)
             done += count
 
     sums = {}
@@ -291,6 +288,8 @@
             to_chip(k).wait_send()
             relay(k).wait_send()
         for step in range(1, group):
+            share(step).wait_send()
+        for step in range(1, group):
             shared(step).wait_recv()
 
     with jax.named_scope('finish'):
@@ -304,9 +303,6 @@
         out_ref[0:1, 0:pairs] = jnp.sum(jnp.where(lane == sub, own, 0.0), axis=0, keepdims=True)[:, :pairs]
         total = jnp.sum(lse_query, axis=1, keepdims=True) + jnp.sum(every[:, 2, :], axis=0, keepdims=True)[:, :1]
         out_ref[2:3, 0:1] = total / (2 * queries)
-
-    for step in range(1, group):
-        share(step).wait_send()
 
 
 def solution(mesh):

time: 32.6 us -> 32.5 us (level)
  no operation moved by 1% of the time
where the time goes in v6:
time: 32.5 us; the launch traced here: 32.4 us
  Pallas kernels  31.2 us (96%)
  between operations  1.29 us (4%)
    pallas_call x1, Pallas kernels, local_loss(): pl.pallas_call(functools.partial(kernel, group), out_shape=[jax.ShapeDtyp...  30.6 us

profile of v6, /device:TPU:21, one launch (start us, length us, event | category | flops | bytes accessed | tf_op | source)
XLA Modules:
  0.0 32.4 jit_solution(14932321132988520256)
XLA Ops:
  1.3 30.6 %late_interaction.1.x_ref = f32[8,128]{1,0:T(8,128)S(1)} custom-call(f32[1]{0:T(128)} %bitcast.8.temp_hbm, bf16[160,1536]{1,0:T(8,128)(2,1)} %bitcast.10, bf16[6144,1536]{1,0:T(8,128)(2,1)} %bitcast.9, bf16[1536,128]{1,0:T(8,128)(2,1)} %w_hbm.1, s32[8,20]{1,0:T(8,128)} %qm_hbm.1, s32[8,768]{1,0:T(8,128)} %dm_hbm.1), custom_call_target="tpu_custom_call" | custom-call | tf_op jit(solution)/shard_map/late_interaction/pallas_call | solution.py:320
  31.9 0.5 %unpack.1 = (f32[1,8]{1,0:T(1,128)}, f32[1,8]{1,0:T(1,128)}, f32[1,1]{1,0:T(1,128)}) custom-call(f32[8,128]{1,0:T(8,128)S(1)} %late_interaction.1.x_ref), custom_call_target="tpu_custom_call" | custom-call | tf_op jit(solution)/shard_map/unpack/pallas_call | solution.py:359
